TPU v7x, 256 devices: a whole 4x4x8 slice. The times are simulated.
256 devices in a mesh: row: 8 (over y, core), col: 4 (over x), layer: 8 (over z).
Axes of the slice: x: 4, y: 4, z: 8, core: 2. Of those that a mesh axis runs over, the one named last changes fastest.
Arguments:
- hamiltonian: bfloat16 [5120, 5120], P(('row', 'layer'), 'col'), may hold values from -1.2 to 1.2, as said below
- tile_pattern: int32 [40, 40], replicated, may hold values from 0 to 1, as said below
- n_occ: int32 [1], replicated, may hold values from 1024 to 4095
- mu: float32 [1], replicated, may hold values from -0.2 to 0.2
- gamma: float32 [1], replicated, may hold values from 0.25 to 0.4
Outputs:
- density: float32 [5120, 5120], P(('row', 'layer'), 'col')
Inputs may be any that keep to these rules, and one draw needn't show every extreme that they name: `tile_pattern`: Symmetric, 0 or 1, with ones on the diagonal and next to it. `hamiltonian`: Symmetric; its eigenvalues lie within -1.8 and 1.8.
All inputs are finite; a program needn't handle non-finite values.
Results may differ from a plain program's by a relative error of at most 0.0055.
Values may be sent and summed in bfloat16 or wider, within the bound.
No kernel may reach another device: no remote copies, remote signals or barrier semaphores. Data moves between devices by JAX's collectives and lax.ppermute only.
A program may use at most 64 MiB of HBM per device.

v0:
```python
import jax
import jax.numpy as jnp
from jax import lax
from jax.sharding import PartitionSpec as P

TILE = 128
STEPS = 2


def element_mask(tile_pattern, row_start, row_count, col_start, col_count):
    tile_count = tile_pattern.shape[0]
    tile_ids = jnp.arange(tile_count, dtype=jnp.int32)
    row_tiles = (row_start + jnp.arange(row_count, dtype=jnp.int32)) // TILE
    col_tiles = (col_start + jnp.arange(col_count, dtype=jnp.int32)) // TILE
    row_hot = (row_tiles[:, None] == tile_ids[None, :]).astype(jnp.bfloat16)
    col_hot = (tile_ids[:, None] == col_tiles[None, :]).astype(jnp.bfloat16)
    picked = jnp.dot(row_hot, tile_pattern.astype(jnp.bfloat16), preferred_element_type=jnp.float32)
    return jnp.dot(picked.astype(jnp.bfloat16), col_hot, preferred_element_type=jnp.float32)


def shards(hamiltonian, tile_pattern, n_occ, mu, gamma):
    share_rows, band_cols = hamiltonian.shape
    n_col = lax.axis_size("col")
    n_layer = lax.axis_size("layer")
    order = band_cols * n_col
    layer_index = lax.axis_index("layer")
    row_start = (lax.axis_index("row") * n_layer + layer_index) * share_rows
    col_start = lax.axis_index("col") * band_cols
    mask = element_mask(tile_pattern, row_start, share_rows, col_start, band_cols)
    row_global = row_start + jnp.arange(share_rows, dtype=jnp.int32)
    col_global = col_start + jnp.arange(band_cols, dtype=jnp.int32)
    identity = (row_global[:, None] == col_global[None, :]).astype(jnp.float32)
    filling = n_occ[0].astype(jnp.float32) / order
    start = mask * (
        filling * identity + gamma[0] * (mu[0] * identity - hamiltonian.astype(jnp.float32))
    )
    current = start.astype(jnp.bfloat16)
    result = start
    for iteration in range(STEPS):
        column = lax.all_gather(current, ("row", "layer"), axis=0, tiled=True)

        def rows_product(left_share):
            return jnp.dot(
                lax.all_gather(left_share, "col", axis=1, tiled=True),
                column,
                preferred_element_type=jnp.float32,
            )

        square = mask * rows_product(current)
        cube = mask * rows_product(square.astype(jnp.bfloat16))
        result = 3.0 * square - 2.0 * cube
        current = result.astype(jnp.bfloat16)
    return result


def solution(mesh):
    placed = (P(("row", "layer"), "col"), P(), P(), P(), P())
    return jax.shard_map(
        shards, mesh=mesh, in_specs=placed, out_specs=P(("row", "layer"), "col"), check_vma=False
    )
```

profile of v0, /device:TPU:2, one launch (start us, length us, event | category | flops | bytes accessed | tf_op | source)
XLA Modules:
  0.0 248.6 jit_solution(11599922052640103232)
XLA Ops:
  6.5 0.0 all-gather.3.cloned.1.call-start
  8.5 2.0 fusion.8
  10.5 0.0 all-gather.3.cloned.1.call-update
  10.6 0.0 all-gather.5.cloned.1.call-start
  10.6 14.4 %all_gather.18 = bf16[80,5120]{1,0:T(8,128)(2,1)S(1)} all-gather(bf16[80,1280]{1,0:T(8,128)(2,1)} %get-tuple-element.5), channel_id=1, replica_groups=mesh['row'=8,'col'=4,'layer'=8] {'col'}, dimensions={1}, use_global_device_ids=true | all-gather | bytes 1024000 | tf_op jit(solution)/shard_map/all_gather | solution.py:44
  25.0 79.3 %all-gather.3.cloned.1.call-done = bf16[5120,1280]{1,0:T(8,128)(2,1)} async-done(((bf16[80,1280]{1,0:T(8,128)(2,1)}), bf16[5120,1280]{1,0:T(8,128)(2,1)}) %all-gather.3.cloned.1.call-update) | async-done | bytes 13107216 | tf_op jit(solution)/shard_map/all_gather | solution.py:40
  104.3 0.0 copy-start
  104.3 7.2 %fusion.21 = (bf16[80,1280]{1,0:T(8,128)(2,1)S(1)}, f32[80,1280]{1,0:T(8,128)S(1)}) fusion(f32[80,1280]{1,0:T(8,128)S(1)} %get-tuple-element.6, bf16[80,5120]{1,0:T(8,128)(2,1)S(1)} %all_gather.18, bf16[5120,1280]{1,0:T(8,128)(2,1)} %all-gather.3.cloned.1.call-done), kind=kOutput, calls=%fused_computation.37 | convolution fusion | flops 1048780800 | bytes 14950400 | tf_op jit(solution)/shard_map/dot_general | solution.py:43
  111.6 14.6 %all_gather.20 = bf16[80,5120]{1,0:T(8,128)(2,1)S(1)} all-gather(bf16[80,1280]{1,0:T(8,128)(2,1)S(1)} %get-tuple-element.7), channel_id=1, replica_groups=mesh['row'=8,'col'=4,'layer'=8] {'col'}, dimensions={1}, use_global_device_ids=true | all-gather | bytes 1024000 | tf_op jit(solution)/shard_map/all_gather | solution.py:44
  126.2 0.0 copy-done
  126.2 3.1 %fusion.4 = bf16[80,1280]{1,0:T(8,128)(2,1)} fusion(f32[80,1280]{1,0:T(8,128)S(1)} %get-tuple-element.6, bf16[80,5120]{1,0:T(8,128)(2,1)S(1)} %all_gather.20, bf16[5120,1280]{1,0:T(8,128)(2,1)S(1)} %copy-done, f32[80,1280]{1,0:T(8,128)S(1)} %get-tuple-element.8), kind=kOutput, calls=%fused_computation.8 | convolution fusion | flops 1049088000 | bytes 14950400 | tf_op jit(solution)/shard_map/dot_general | solution.py:43
  129.2 0.0 all-gather.5.cloned.1.call-update
  129.3 13.6 %all_gather.21 = bf16[80,5120]{1,0:T(8,128)(2,1)S(1)} all-gather(bf16[80,1280]{1,0:T(8,128)(2,1)} %fusion.4), channel_id=1, replica_groups=mesh['row'=8,'col'=4,'layer'=8] {'col'}, dimensions={1}, use_global_device_ids=true | all-gather | bytes 1024000 | tf_op jit(solution)/shard_map/all_gather | solution.py:44
  142.8 73.9 %all-gather.5.cloned.1.call-done = bf16[5120,1280]{1,0:T(8,128)(2,1)} async-done(((bf16[80,1280]{1,0:T(8,128)(2,1)}), bf16[5120,1280]{1,0:T(8,128)(2,1)}) %all-gather.5.cloned.1.call-update) | async-done | bytes 13107216 | tf_op jit(solution)/shard_map/all_gather | solution.py:40
  216.7 0.0 copy-start.1
  216.8 7.2 %fusion.22 = (bf16[80,1280]{1,0:T(8,128)(2,1)S(1)}, f32[80,1280]{1,0:T(8,128)S(1)}) fusion(f32[80,1280]{1,0:T(8,128)S(1)} %get-tuple-element.6, bf16[80,5120]{1,0:T(8,128)(2,1)S(1)} %all_gather.21, bf16[5120,1280]{1,0:T(8,128)(2,1)} %all-gather.5.cloned.1.call-done), kind=kOutput, calls=%fused_computation.38 | convolution fusion | flops 1048780800 | bytes 14950400 | tf_op jit(solution)/shard_map/dot_general | solution.py:43
  224.0 14.6 %all_gather.23 = bf16[80,5120]{1,0:T(8,128)(2,1)S(1)} all-gather(bf16[80,1280]{1,0:T(8,128)(2,1)S(1)} %get-tuple-element.9), channel_id=1, replica_groups=mesh['row'=8,'col'=4,'layer'=8] {'col'}, dimensions={1}, use_global_device_ids=true | all-gather | bytes 1024000 | tf_op jit(solution)/shard_map/all_gather | solution.py:44
  238.6 0.0 copy-done.1
  238.6 3.1 %fusion.2 = f32[80,1280]{1,0:T(8,128)} fusion(f32[80,1280]{1,0:T(8,128)S(1)} %get-tuple-element.6, bf16[80,5120]{1,0:T(8,128)(2,1)S(1)} %all_gather.23, bf16[5120,1280]{1,0:T(8,128)(2,1)S(1)} %copy-done.1, f32[80,1280]{1,0:T(8,128)S(1)} %get-tuple-element.10), kind=kOutput, calls=%fused_computation.6 | convolution fusion | flops 1048985600 | bytes 15155200 | tf_op jit(solution)/shard_map/dot_general | solution.py:43
  (2 shorter events, 0.0 us)
Async XLA Ops:
  6.5 97.8 %all-gather.3.cloned.1.call-start = ((), (), s32[]{:S(2)}) async-start(), calls=%async_computation | async-start | bytes 13312000 | tf_op jit(solution)/shard_map/all_gather | solution.py:40
  10.6 206.2 %all-gather.5.cloned.1.call-start = ((), (), s32[]{:S(2)}) async-start(), calls=%async_computation.1 | async-start | bytes 13312000 | tf_op jit(solution)/shard_map/all_gather | solution.py:40
  104.3 21.9 %copy-start = (bf16[5120,1280]{1,0:T(8,128)(2,1)S(1)}, bf16[5120,1280]{1,0:T(8,128)(2,1)}, u32[]{:S(2)}) copy-start(bf16[5120,1280]{1,0:T(8,128)(2,1)} %all-gather.3.cloned.1.call-done) | copy-start | bytes 39321604
  216.7 21.8 %copy-start.1 = (bf16[5120,1280]{1,0:T(8,128)(2,1)S(1)}, bf16[5120,1280]{1,0:T(8,128)(2,1)}, u32[]{:S(2)}) copy-start(bf16[5120,1280]{1,0:T(8,128)(2,1)} %all-gather.5.cloned.1.call-done) | copy-start | bytes 39321604
Sparse Core Ops, SparseCore 0:
  10.7 93.5 all-gather.2
  129.4 87.3 all-gather.4
where the time goes:
time: 249 us
  waiting for transfers between devices  153 us (61%)
  blocking collectives  57.2 us (23%)
  matrix products  22.7 us (9%)
  between operations  15.4 us (6%)
    all_gather x2, waiting for transfers between devices, shards(): column = lax.all_gather(current, ('row', 'layer'), axis=0, tiled=True)  153 us
    all_gather x4, blocking collectives, rows_product(): lax.all_gather(left_share, 'col', axis=1, tiled=True)  57.2 us
    dot_general x4, matrix products, rows_product(): jnp.dot(lax.all_gather(left_share, 'col', axis=1, tiled=True), column, pr...  20.7 us
  transfers between devices with their start and end apart: 2, of which 2 were waited for; matrix products, arithmetic and copies ran while one was open for 0% of the time, Pallas kernels for 0%

commit v1 on v0

--- a/solution.py
+++ b/solution.py
@@ -5,6 +5,28 @@
 
 TILE = 128
 STEPS = 2
+
+
+def laid_out(pieces, dim):
+    lengths = list(pieces.shape[1:])
+    lengths[dim] *= pieces.shape[0]
+    return jnp.moveaxis(pieces, 0, dim).reshape(lengths)
+
+
+def ring_gather(x, axis, dim):
+    length = lax.axis_size(axis)
+    pairs = [(i, (i + 1) % length) for i in range(length)]
+    back = [(b, a) for a, b in pairs]
+    lower, upper = ([], [])
+    for turn in range(length - 1):
+        if turn % 2 == 0:
+            lower.append(lax.ppermute(lower[-1] if lower else x, axis, pairs))
+        else:
+            upper.append(lax.ppermute(upper[-1] if upper else x, axis, back))
+    tiles = jnp.stack([*lower[::-1], x, *upper])
+    shift = lax.axis_index(axis) - len(lower)
+    tiles = tiles[(jnp.arange(length) - shift) % length]
+    return laid_out(tiles, dim)
 
 
 def element_mask(tile_pattern, row_start, row_count, col_start, col_count):
@@ -41,9 +63,7 @@
 
         def rows_product(left_share):
             return jnp.dot(
-                lax.all_gather(left_share, "col", axis=1, tiled=True),
-                column,
-                preferred_element_type=jnp.float32,
+                ring_gather(left_share, "col", 1), column, preferred_element_type=jnp.float32
             )
 
         square = mask * rows_product(current)

time: 249 us -> 260 us (1.044)
  blocking collectives: 57.2 us -> 0 us
  waiting for transfers between devices: 153 us -> 191 us
  starting transfers between devices: 0.04 us -> 14.7 us
  matrix products: 22.7 us -> 31.9 us
  local copies, waits for them, and re-layouts: 0.01 us -> 2.64 us
    all_gather x4 -> x0, blocking collectives: 57.2 us -> none  [rows_product(): lax.all_gather(left_share, 'col', axis=1, tiled=True)]
    ppermute x0 -> x12, waiting for transfers between devices: none -> 39.9 us  [the longest x8 39.9 us: ring_gather(): lower.append(lax.ppermute(lower[-1] if lower else x, axis, pairs))]
    ppermute x0 -> x12, starting transfers between devices: none -> 14.6 us  [the longest x8 11.1 us: ring_gather(): lower.append(lax.ppermute(lower[-1] if lower else x, axis, pairs))]
    dot_general x4, matrix products: 20.7 us -> 29.8 us  [rows_product(): jnp.dot(ring_gather(left_share, 'col', 1), column, preferred_element_type...]
  transfers between devices with their start and end apart: 2 -> 14, of which waited for: 2 -> 10; matrix products, arithmetic and copies ran while one was open for 0% -> 1% of each run, Pallas kernels for 0% -> 0%
where the time goes in v1:
time: 260 us; the launch traced here: 258 us
  waiting for transfers between devices  191 us (73%)
  matrix products  31.9 us (12%)
  between operations  15.5 us (6%)
  starting transfers between devices  14.7 us (6%)
  local copies, waits for them, and re-layouts  2.64 us (1%)
    all_gather x2, waiting for transfers between devices, shards(): column = lax.all_gather(current, ('row', 'layer'), axis=0, tiled=True)  151 us
    ppermute x8, waiting for transfers between devices, ring_gather(): lower.append(lax.ppermute(lower[-1] if lower else x, axis, pairs))  39.9 us
    dot_general x4, matrix products, rows_product(): jnp.dot(ring_gather(left_share, 'col', 1), column, preferred_element_type...  29.8 us
    ppermute x8, starting transfers between devices, ring_gather(): lower.append(lax.ppermute(lower[-1] if lower else x, axis, pairs))  11.1 us
  transfers between devices with their start and end apart: 14, of which 10 were waited for; matrix products, arithmetic and copies ran while one was open for 1% of the time, Pallas kernels for 0%

profile of v1, /device:TPU:2, one launch (start us, length us, event | category | flops | bytes accessed | tf_op | source)
XLA Modules:
  0.0 257.8 jit_solution(14285584119065555538)
XLA Ops:
  6.5 0.0 all-gather.3.cloned.1.call-start
  8.5 2.0 fusion.8
  10.5 0.0 all-gather.3.cloned.1.call-update
  10.6 0.0 all-gather.5.cloned.1.call-start
  10.6 1.6 collective-permute-start
  12.2 0.8 collective-permute-start.2
  13.0 4.7 %collective-permute-done = bf16[80,1280]{1,0:T(8,128)(2,1)S(1)} collective-permute-done((bf16[80,1280]{1,0:T(8,128)(2,1)}, bf16[80,1280]{1,0:T(8,128)(2,1)S(1)}, u32[]{:S(2)}, u32[]{:S(2)}) %collective-permute-start) | collective-permute-done | bytes 204832 | tf_op jit(solution)/shard_map/ppermute | solution.py:23
  17.7 1.5 collective-permute-start.1
  19.2 0.0 collective-permute-done.2
  19.2 4.6 %collective-permute-done.1 = bf16[80,1280]{1,0:T(8,128)(2,1)S(1)} collective-permute-done((bf16[80,1280]{1,0:T(8,128)(2,1)S(1)}, bf16[80,1280]{1,0:T(8,128)(2,1)S(1)}, u32[]{:S(2)}, u32[]{:S(2)}) %collective-permute-start.1) | collective-permute-done | bytes 204832 | tf_op jit(solution)/shard_map/ppermute | solution.py:23
  23.8 1.0 pad_maximum_fusion
  24.9 0.6 gather_fusion
  25.5 0.1 copy.10
  25.6 78.8 %all-gather.3.cloned.1.call-done = bf16[5120,1280]{1,0:T(8,128)(2,1)} async-done(((bf16[80,1280]{1,0:T(8,128)(2,1)}), bf16[5120,1280]{1,0:T(8,128)(2,1)}) %all-gather.3.cloned.1.call-update) | async-done | bytes 13107216 | tf_op jit(solution)/shard_map/all_gather | solution.py:62
  104.3 7.1 %fusion.23 = (bf16[80,1280]{1,0:T(8,128)(2,1)S(1)}, f32[80,1280]{1,0:T(8,128)S(1)}) fusion(f32[80,1280]{1,0:T(8,128)S(1)} %get-tuple-element.6, bf16[80,5120]{1,0:T(8,128)(2,1)S(1)} %bitcast.43, bf16[5120,1280]{1,0:T(8,128)(2,1)} %all-gather.3.cloned.1.call-done), kind=kOutput, calls=%fused_computation.52 | convolution fusion | flops 1048780800 | bytes 14950400 | tf_op jit(solution)/shard_map/dot_general | solution.py:65
  111.4 1.5 collective-permute-start.3
  113.0 0.6 collective-permute-start.5
  113.5 5.2 %collective-permute-done.3 = bf16[80,1280]{1,0:T(8,128)(2,1)S(1)} collective-permute-done((bf16[80,1280]{1,0:T(8,128)(2,1)S(1)}, bf16[80,1280]{1,0:T(8,128)(2,1)S(1)}, u32[]{:S(2)}, u32[]{:S(2)}) %collective-permute-start.3) | collective-permute-done | bytes 204832 | tf_op jit(solution)/shard_map/ppermute | solution.py:23
  118.7 1.5 collective-permute-start.4
  120.2 0.0 collective-permute-done.5
  120.2 4.9 %collective-permute-done.4 = bf16[80,1280]{1,0:T(8,128)(2,1)S(1)} collective-permute-done((bf16[80,1280]{1,0:T(8,128)(2,1)S(1)}, bf16[80,1280]{1,0:T(8,128)(2,1)S(1)}, u32[]{:S(2)}, u32[]{:S(2)}) %collective-permute-start.4) | collective-permute-done | bytes 204832 | tf_op jit(solution)/shard_map/ppermute | solution.py:23
  125.1 0.1 pad_maximum_fusion.1
  125.2 0.6 gather_fusion.1
  125.8 0.1 copy.11
  125.9 7.8 %fusion.4 = bf16[80,1280]{1,0:T(8,128)(2,1)} fusion(f32[80,1280]{1,0:T(8,128)S(1)} %get-tuple-element.6, bf16[80,5120]{1,0:T(8,128)(2,1)S(1)} %bitcast.46, bf16[5120,1280]{1,0:T(8,128)(2,1)} %all-gather.3.cloned.1.call-done, f32[80,1280]{1,0:T(8,128)S(1)} %get-tuple-element.8), kind=kOutput, calls=%fused_computation.12 | convolution fusion | flops 1049088000 | bytes 14950400 | tf_op jit(solution)/shard_map/dot_general | solution.py:65
  133.7 0.0 all-gather.5.cloned.1.call-update
  133.7 1.5 collective-permute-start.6
  135.2 1.6 collective-permute-start.8
  136.8 3.9 %collective-permute-done.6 = bf16[80,1280]{1,0:T(8,128)(2,1)S(1)} collective-permute-done((bf16[80,1280]{1,0:T(8,128)(2,1)}, bf16[80,1280]{1,0:T(8,128)(2,1)S(1)}, u32[]{:S(2)}, u32[]{:S(2)}) %collective-permute-start.6) | collective-permute-done | bytes 204832 | tf_op jit(solution)/shard_map/ppermute | solution.py:23
  140.7 0.5 collective-permute-start.7
  141.2 0.0 collective-permute-done.8
  141.2 6.5 %collective-permute-done.7 = bf16[80,1280]{1,0:T(8,128)(2,1)S(1)} collective-permute-done((bf16[80,1280]{1,0:T(8,128)(2,1)S(1)}, bf16[80,1280]{1,0:T(8,128)(2,1)S(1)}, u32[]{:S(2)}, u32[]{:S(2)}) %collective-permute-start.7) | collective-permute-done | bytes 204832 | tf_op jit(solution)/shard_map/ppermute | solution.py:23
  147.7 1.0 pad_maximum_fusion.2
  148.7 0.6 gather_fusion.2
  149.3 0.1 copy.12
  149.4 72.1 %all-gather.5.cloned.1.call-done = bf16[5120,1280]{1,0:T(8,128)(2,1)} async-done(((bf16[80,1280]{1,0:T(8,128)(2,1)}), bf16[5120,1280]{1,0:T(8,128)(2,1)}) %all-gather.5.cloned.1.call-update) | async-done | bytes 13107216 | tf_op jit(solution)/shard_map/all_gather | solution.py:62
  221.5 7.1 %fusion.24 = (bf16[80,1280]{1,0:T(8,128)(2,1)S(1)}, f32[80,1280]{1,0:T(8,128)S(1)}) fusion(f32[80,1280]{1,0:T(8,128)S(1)} %get-tuple-element.6, bf16[80,5120]{1,0:T(8,128)(2,1)S(1)} %bitcast.44, bf16[5120,1280]{1,0:T(8,128)(2,1)} %all-gather.5.cloned.1.call-done), kind=kOutput, calls=%fused_computation.53 | convolution fusion | flops 1048780800 | bytes 14950400 | tf_op jit(solution)/shard_map/dot_general | solution.py:65
  228.6 1.5 collective-permute-start.9
  230.1 0.6 collective-permute-start.11
  230.7 5.2 %collective-permute-done.9 = bf16[80,1280]{1,0:T(8,128)(2,1)S(1)} collective-permute-done((bf16[80,1280]{1,0:T(8,128)(2,1)S(1)}, bf16[80,1280]{1,0:T(8,128)(2,1)S(1)}, u32[]{:S(2)}, u32[]{:S(2)}) %collective-permute-start.9) | collective-permute-done | bytes 204832 | tf_op jit(solution)/shard_map/ppermute | solution.py:23
  235.9 1.5 collective-permute-start.10
  237.4 0.0 collective-permute-done.11
  237.4 4.9 %collective-permute-done.10 = bf16[80,1280]{1,0:T(8,128)(2,1)S(1)} collective-permute-done((bf16[80,1280]{1,0:T(8,128)(2,1)S(1)}, bf16[80,1280]{1,0:T(8,128)(2,1)S(1)}, u32[]{:S(2)}, u32[]{:S(2)}) %collective-permute-start.10) | collective-permute-done | bytes 204832 | tf_op jit(solution)/shard_map/ppermute | solution.py:23
  242.3 0.1 pad_maximum_fusion.3
  242.4 0.6 gather_fusion.3
  243.0 0.1 copy.13
  243.1 7.9 %fusion.2 = f32[80,1280]{1,0:T(8,128)} fusion(f32[80,1280]{1,0:T(8,128)S(1)} %get-tuple-element.6, bf16[80,5120]{1,0:T(8,128)(2,1)S(1)} %bitcast.45, bf16[5120,1280]{1,0:T(8,128)(2,1)} %all-gather.5.cloned.1.call-done, f32[80,1280]{1,0:T(8,128)S(1)} %get-tuple-element.10), kind=kOutput, calls=%fused_computation.10 | convolution fusion | flops 1048985600 | bytes 15155200 | tf_op jit(solution)/shard_map/dot_general | solution.py:65
  (4 shorter events, 0.0 us)
Async XLA Ops:
  6.5 97.8 %all-gather.3.cloned.1.call-start = ((), (), s32[]{:S(2)}) async-start(), calls=%async_computation | async-start | bytes 13312000 | tf_op jit(solution)/shard_map/all_gather | solution.py:62
  10.6 210.9 %all-gather.5.cloned.1.call-start = ((), (), s32[]{:S(2)}) async-start(), calls=%async_computation.1 | async-start | bytes 13312000 | tf_op jit(solution)/shard_map/all_gather | solution.py:62
  10.6 7.1 %collective-permute-start = (bf16[80,1280]{1,0:T(8,128)(2,1)}, bf16[80,1280]{1,0:T(8,128)(2,1)S(1)}, u32[]{:S(2)}, u32[]{:S(2)}) collective-permute-start(bf16[80,1280]{1,0:T(8,128)(2,1)} %get-tuple-element.5), channel_id=1, source_target_pairs={{0,8},{8,16},{16,24},{24,0},{1,9},{9,17},{17,25},{25,1},{2,10},{10... | collective-permute-start | bytes 614408 | tf_op jit(solution)/shard_map/ppermute | solution.py:23
  12.2 7.1 %collective-permute-start.2 = (bf16[80,1280]{1,0:T(8,128)(2,1)}, bf16[80,1280]{1,0:T(8,128)(2,1)S(1)}, u32[]{:S(2)}, u32[]{:S(2)}) collective-permute-start(bf16[80,1280]{1,0:T(8,128)(2,1)} %get-tuple-element.5), channel_id=1, source_target_pairs={{8,0},{16,8},{24,16},{0,24},{9,1},{17,9},{25,17},{1,25},{10,2},{18... | collective-permute-start | bytes 614408 | tf_op jit(solution)/shard_map/ppermute | solution.py:25
  17.7 6.1 %collective-permute-start.1 = (bf16[80,1280]{1,0:T(8,128)(2,1)S(1)}, bf16[80,1280]{1,0:T(8,128)(2,1)S(1)}, u32[]{:S(2)}, u32[]{:S(2)}) collective-permute-start(bf16[80,1280]{1,0:T(8,128)(2,1)S(1)} %collective-permute-done), channel_id=1, source_target_pairs={{0,8},{8,16},{16,24},{24,0},{1,9},{9,17},{17,25},{25,1},{2,10},{10... | collective-permute-start | bytes 614408 | tf_op jit(solution)/shard_map/ppermute | solution.py:23
  111.4 7.3 %collective-permute-start.3 = (bf16[80,1280]{1,0:T(8,128)(2,1)S(1)}, bf16[80,1280]{1,0:T(8,128)(2,1)S(1)}, u32[]{:S(2)}, u32[]{:S(2)}) collective-permute-start(bf16[80,1280]{1,0:T(8,128)(2,1)S(1)} %get-tuple-element.7), channel_id=1, source_target_pairs={{0,8},{8,16},{16,24},{24,0},{1,9},{9,17},{17,25},{25,1},{2,10},{10... | collective-permute-start | bytes 614408 | tf_op jit(solution)/shard_map/ppermute | solution.py:23
  113.0 7.2 %collective-permute-start.5 = (bf16[80,1280]{1,0:T(8,128)(2,1)S(1)}, bf16[80,1280]{1,0:T(8,128)(2,1)S(1)}, u32[]{:S(2)}, u32[]{:S(2)}) collective-permute-start(bf16[80,1280]{1,0:T(8,128)(2,1)S(1)} %get-tuple-element.7), channel_id=1, source_target_pairs={{8,0},{16,8},{24,16},{0,24},{9,1},{17,9},{25,17},{1,25},{10,2},{18... | collective-permute-start | bytes 614408 | tf_op jit(solution)/shard_map/ppermute | solution.py:25
  118.7 6.4 %collective-permute-start.4 = (bf16[80,1280]{1,0:T(8,128)(2,1)S(1)}, bf16[80,1280]{1,0:T(8,128)(2,1)S(1)}, u32[]{:S(2)}, u32[]{:S(2)}) collective-permute-start(bf16[80,1280]{1,0:T(8,128)(2,1)S(1)} %collective-permute-done.3), channel_id=1, source_target_pairs={{0,8},{8,16},{16,24},{24,0},{1,9},{9,17},{17,25},{25,1},{2,10},{10... | collective-permute-start | bytes 614408 | tf_op jit(solution)/shard_map/ppermute | solution.py:23
  133.7 7.0 %collective-permute-start.6 = (bf16[80,1280]{1,0:T(8,128)(2,1)}, bf16[80,1280]{1,0:T(8,128)(2,1)S(1)}, u32[]{:S(2)}, u32[]{:S(2)}) collective-permute-start(bf16[80,1280]{1,0:T(8,128)(2,1)} %fusion.4), channel_id=1, source_target_pairs={{0,8},{8,16},{16,24},{24,0},{1,9},{9,17},{17,25},{25,1},{2,10},{10... | collective-permute-start | bytes 614408 | tf_op jit(solution)/shard_map/ppermute | solution.py:23
  135.2 6.0 %collective-permute-start.8 = (bf16[80,1280]{1,0:T(8,128)(2,1)}, bf16[80,1280]{1,0:T(8,128)(2,1)S(1)}, u32[]{:S(2)}, u32[]{:S(2)}) collective-permute-start(bf16[80,1280]{1,0:T(8,128)(2,1)} %fusion.4), channel_id=1, source_target_pairs={{8,0},{16,8},{24,16},{0,24},{9,1},{17,9},{25,17},{1,25},{10,2},{18... | collective-permute-start | bytes 614408 | tf_op jit(solution)/shard_map/ppermute | solution.py:25
  140.7 6.9 %collective-permute-start.7 = (bf16[80,1280]{1,0:T(8,128)(2,1)S(1)}, bf16[80,1280]{1,0:T(8,128)(2,1)S(1)}, u32[]{:S(2)}, u32[]{:S(2)}) collective-permute-start(bf16[80,1280]{1,0:T(8,128)(2,1)S(1)} %collective-permute-done.6), channel_id=1, source_target_pairs={{0,8},{8,16},{16,24},{24,0},{1,9},{9,17},{17,25},{25,1},{2,10},{10... | collective-permute-start | bytes 614408 | tf_op jit(solution)/shard_map/ppermute | solution.py:23
  228.6 7.3 %collective-permute-start.9 = (bf16[80,1280]{1,0:T(8,128)(2,1)S(1)}, bf16[80,1280]{1,0:T(8,128)(2,1)S(1)}, u32[]{:S(2)}, u32[]{:S(2)}) collective-permute-start(bf16[80,1280]{1,0:T(8,128)(2,1)S(1)} %get-tuple-element.9), channel_id=1, source_target_pairs={{0,8},{8,16},{16,24},{24,0},{1,9},{9,17},{17,25},{25,1},{2,10},{10... | collective-permute-start | bytes 614408 | tf_op jit(solution)/shard_map/ppermute | solution.py:23
  230.1 7.2 %collective-permute-start.11 = (bf16[80,1280]{1,0:T(8,128)(2,1)S(1)}, bf16[80,1280]{1,0:T(8,128)(2,1)S(1)}, u32[]{:S(2)}, u32[]{:S(2)}) collective-permute-start(bf16[80,1280]{1,0:T(8,128)(2,1)S(1)} %get-tuple-element.9), channel_id=1, source_target_pairs={{8,0},{16,8},{24,16},{0,24},{9,1},{17,9},{25,17},{1,25},{10,2},{18... | collective-permute-start | bytes 614408 | tf_op jit(solution)/shard_map/ppermute | solution.py:25
  235.9 6.4 %collective-permute-start.10 = (bf16[80,1280]{1,0:T(8,128)(2,1)S(1)}, bf16[80,1280]{1,0:T(8,128)(2,1)S(1)}, u32[]{:S(2)}, u32[]{:S(2)}) collective-permute-start(bf16[80,1280]{1,0:T(8,128)(2,1)S(1)} %collective-permute-done.9), channel_id=1, source_target_pairs={{0,8},{8,16},{16,24},{24,0},{1,9},{9,17},{17,25},{25,1},{2,10},{10... | collective-permute-start | bytes 614408 | tf_op jit(solution)/shard_map/ppermute | solution.py:23
Sparse Core Ops, SparseCore 0:
  10.7 93.5 all-gather.2
  133.8 87.6 all-gather.4
